TPU v7x, 32 devices: a whole 2x2x4 slice. The times are simulated.
32 devices in a mesh: expert: 4 (over y, x), tensor: 4 (over z), rep: 2 (over core).
Axes of the slice: x: 2, y: 2, z: 4, core: 2. Of those that a mesh axis runs over, the one named last changes fastest.
Arguments:
- requests: bfloat16 [512, 1536], P('expert', ('tensor', 'rep')), may hold values from -6 to 6
- expert_ids: int32 [512, 2], P('expert'), may hold values from 0 to 3, all different within a row; in each aligned block of 128 rows (0 to 127, 128 to 255, ...) at most 96 rows name the same one
- gate_values: float32 [512, 2], P('expert'), may hold values from 0.2 to 1
- w_up: bfloat16 [4, 1536, 6144], P(None, 'expert', ('tensor', 'rep')), may hold values from -0.15625 to 0.15625
- w_down: bfloat16 [4, 1536, 6144], P(None, 'expert', ('tensor', 'rep')), may hold values from -0.078125 to 0.078125
- tower_in: bfloat16 [1536, 768], P(('tensor', 'rep')), may hold values from -0.15625 to 0.15625
- tower_bias: float32 [768], replicated, may hold values from -3 to 3
- tower_out: float32 [3, 256], replicated, may hold values from -0.375 to 0.375
- out_bias: float32 [3], replicated, may hold values from -3 to 3
Outputs:
- mixed: bfloat16 [512, 1536], P('expert', ('tensor', 'rep'))
- scores: float32 [3, 512], P(None, ('expert', 'tensor', 'rep'))
Inputs may be any that keep to these rules, and one draw needn't show every extreme that they name: `expert_ids`: each row names two different experts. In the rows of one device (128 requests) no expert is named more than 96 times, a bound that some block reaches.
All inputs are finite; a program needn't handle non-finite values.
Results may differ from a plain program's by a relative error of at most 0.015.
Values may be sent and summed in bfloat16 or wider, within the bound.
No kernel may reach another device: no remote copies, remote signals or barrier semaphores. Data moves between devices by JAX's collectives and lax.ppermute only.
A program may use at most 64 MiB of HBM per device.

v0:
```python
import jax
import jax.numpy as jnp
from jax import lax
from jax.sharding import PartitionSpec as P


def tower_head(pre, tower_bias, tower_out, out_bias):
    active = jax.nn.relu(pre + tower_bias[None, :])
    active = active.reshape(pre.shape[0], tower_out.shape[0], tower_out.shape[1])
    logits = jnp.sum(active * tower_out[None, :, :], axis=2) + out_bias[None, :]
    return jax.nn.sigmoid(logits).T


def per_device(
    requests, expert_ids, gate_values, w_up, w_down, tower_in, tower_bias, tower_out, out_bias
):
    groups = lax.axis_size("expert")
    experts = w_up.shape[0]
    local_experts = experts // groups
    tok_rows = requests.shape[0]
    capacity = 3 * tok_rows // experts
    serve_up, serve_down = (
        lax.all_to_all(w_up, "expert", split_axis=0, concat_axis=1, tiled=True),
        lax.all_to_all(w_down, "expert", split_axis=0, concat_axis=1, tiled=True),
    )
    flat_ids = expert_ids.reshape(-1)
    onehot = (flat_ids[:, None] == jnp.arange(experts, dtype=jnp.int32)[None, :]).astype(jnp.int32)
    before = jnp.cumsum(onehot, axis=0) - onehot
    slot_rank = jnp.sum(before * onehot, axis=1)
    slots = (flat_ids * capacity + slot_rank).reshape(tok_rows, 2)
    slot_index = jnp.arange(experts * capacity, dtype=jnp.int32)
    spread = (
        (slot_index[:, None] == slots[None, :, 0]) | (slot_index[:, None] == slots[None, :, 1])
    ).astype(jnp.bfloat16)
    full_rows = lax.all_gather(requests, ("tensor", "rep"), axis=1, tiled=True)
    outgoing = jnp.dot(spread, full_rows, preferred_element_type=jnp.float32).astype(jnp.bfloat16)
    incoming = lax.all_to_all(outgoing, "expert", split_axis=0, concat_axis=0, tiled=True)
    shaped = incoming.reshape(groups, local_experts, capacity, incoming.shape[1])
    hidden_pre = jnp.einsum("secd,edh->sech", shaped, serve_up, preferred_element_type=jnp.float32)
    hidden = jax.nn.relu(hidden_pre).astype(jnp.bfloat16)
    partial_value = jnp.einsum(
        "sech,edh->secd", hidden, serve_down, preferred_element_type=jnp.float32
    )
    summed = lax.psum_scatter(
        partial_value.astype(jnp.bfloat16), ("tensor", "rep"), scatter_dimension=3, tiled=True
    ).astype(jnp.float32)
    expert_out = summed.astype(jnp.bfloat16).reshape(
        groups * local_experts * capacity, summed.shape[3]
    )
    returned = lax.all_to_all(expert_out, "expert", split_axis=0, concat_axis=0, tiled=True)
    pick_first = (slots[:, 0:1] == slot_index[None, :]).astype(jnp.bfloat16)
    pick_second = (slots[:, 1:2] == slot_index[None, :]).astype(jnp.bfloat16)
    first = jnp.dot(pick_first, returned, preferred_element_type=jnp.float32)
    second = jnp.dot(pick_second, returned, preferred_element_type=jnp.float32)
    mixed = (gate_values[:, 0:1] * first + gate_values[:, 1:2] * second).astype(jnp.bfloat16)
    pre = lax.psum_scatter(
        jnp.dot(mixed, tower_in, preferred_element_type=jnp.float32).astype(jnp.bfloat16),
        ("tensor", "rep"),
        scatter_dimension=0,
        tiled=True,
    ).astype(jnp.float32)
    scores = tower_head(pre, tower_bias, tower_out, out_bias)
    return (mixed, scores)


def solution(mesh):
    in_specs = (
        P("expert", ("tensor", "rep")),
        P("expert", None),
        P("expert", None),
        P(None, "expert", ("tensor", "rep")),
        P(None, "expert", ("tensor", "rep")),
        P(("tensor", "rep"), None),
        P(),
        P(),
        P(),
    )
    out_specs = (P("expert", ("tensor", "rep")), P(None, ("expert", "tensor", "rep")))
    return jax.shard_map(
        per_device, mesh=mesh, in_specs=in_specs, out_specs=out_specs, check_vma=False
    )
```

profile of v0, /device:TPU:0, one launch (start us, length us, event | category | flops | bytes accessed | tf_op | source)
XLA Modules:
  0.0 198.6 jit_solution(8744839714044765721)
XLA Ops:
  7.2 0.0 copy-start
  7.2 0.0 reduce-scatter.7.cloned.1.call-start
  7.2 0.8 copy.32
  8.0 0.1 eq.85
  8.2 0.1 eq.81
  8.3 1.2 reduce-window.6
  9.6 0.1 slice.26
  9.6 0.1 copy.34
  9.8 0.1 copy.35
  9.9 0.1 add_bitcast_fusion
  10.0 0.1 reduce_sum.21
  10.1 0.1 copy.36
  10.2 0.7 multiply_add_fusion
  10.9 16.4 %all_gather.3 = bf16[128,1536]{0,1:T(8,128)(2,1)S(1)} all-gather(bf16[128,192]{0,1:T(8,128)(2,1)} %param.9), channel_id=1, replica_groups=mesh['expert'=4,'tensor'=4,'rep'=2] {'tensor','rep'}, dimensions={1}, use_global_device_ids=true | all-gather | bytes 442368 | tf_op jit(solution)/shard_map/all_gather | solution.py:35
  27.3 0.5 convolution_convert_fusion
  27.8 0.0 copy-start.1
  27.8 19.8 %all_to_all.39 = bf16[4,96,1536]{2,1,0:T(8,128)(2,1)} all-to-all(bf16[4,96,1536]{2,1,0:T(8,128)(2,1)S(1)} %bitcast.56), channel_id=1, replica_groups=mesh['expert'=4,'tensor'=4,'rep'=2] {'expert'}, dimensions={0} | all-to-all | bytes 2359296 | tf_op jit(solution)/shard_map/all_to_all | solution.py:37
  47.6 0.0 copy-done.1
  47.6 30.1 %all_to_all.40 = bf16[4,384,768]{2,1,0:T(8,128)(2,1)S(1)} all-to-all(bf16[4,384,768]{2,1,0:T(8,128)(2,1)S(1)} %copy-done.1), channel_id=1, replica_groups=mesh['expert'=4,'tensor'=4,'rep'=2] {'expert'}, dimensions={0} | all-to-all | bytes 4718592 | tf_op jit(solution)/shard_map/all_to_all | solution.py:23
  77.7 0.0 copy-done.2
  77.7 29.5 %all_to_all.41 = bf16[4,384,768]{2,1,0:T(8,128)(2,1)} all-to-all(bf16[4,384,768]{2,1,0:T(8,128)(2,1)S(1)} %copy-done.2), channel_id=1, replica_groups=mesh['expert'=4,'tensor'=4,'rep'=2] {'expert'}, dimensions={0} | all-to-all | bytes 4718592 | tf_op jit(solution)/shard_map/all_to_all | solution.py:24
  107.3 5.5 %fusion = bf16[4,1,96,1536]{3,2,0,1:T(8,128)(2,1)} fusion(bf16[1536,768,1]{1,0,2:T(8,128)(2,1)} %bitcast.58, bf16[4,96,1536]{2,1,0:T(8,128)(2,1)} %all_to_all.39, bf16[1536,768,1]{1,0,2:T(8,128)(2,1)S(1)} %bitcast.57), kind=kOutput, calls=%fused_computation.2 | convolution fusion | flops 1813118976 | bytes 7077888 | tf_op jit(solution)/shard_map/sech,edh->secd/dot_general | solution.py:41
  112.7 2.6 %copy.38 = bf16[4,1,96,1536]{2,0,1,3:T(4,128)(2,1)S(1)} copy(bf16[4,1,96,1536]{3,2,0,1:T(8,128)(2,1)} %fusion) | data formatting | bytes 2359296
  115.4 1.9 reshape.69
  117.3 0.0 reduce-scatter.7.cloned.1.call-update
  117.3 0.0 copy-start.5
  117.3 0.0 copy-start.7
  117.3 32.7 %reduce-scatter.7.cloned.1.call-done = bf16[192,384]{1,0:T(8,128)(2,1)} async-done(((bf16[1536,384]{1,0:T(8,128)(2,1)}), bf16[192,384]{1,0:T(8,128)(2,1)}) %reduce-scatter.7.cloned.1.call-update) | async-done | bytes 147472
  150.0 1.1 reshape.70
  151.0 0.8 copy.39
  151.9 3.6 %all-to-all-start.3 = ((bf16[4,96,192]{2,1,0:T(8,128)(2,1)}), bf16[4,96,192]{2,1,0:T(8,128)(2,1)S(1)}, u32[]{:S(2)}, u32[]{:S(2)}) async-start(bf16[4,96,192]{2,1,0:T(8,128)(2,1)} %bitcast.13), calls=%async_computation.3 | async-start | bytes 393216 | tf_op jit(solution)/shard_map/all_to_all | solution.py:50
  155.5 0.0 reduce-scatter.5.cloned.1.call-start
  155.5 0.0 copy-done.6
  155.5 5.2 %all-to-all-done.3 = bf16[4,96,192]{2,1,0:T(8,128)(2,1)S(1)} async-done(((bf16[4,96,192]{2,1,0:T(8,128)(2,1)}), bf16[4,96,192]{2,1,0:T(8,128)(2,1)S(1)}, u32[]{:S(2)}, u32[]{:S(2)}) %all-to-all-start.3) | async-done | bytes 147488 | tf_op jit(solution)/shard_map/all_to_all | solution.py:50
  160.7 0.3 convolution_multiply_fusion
  161.0 0.3 fusion.3
  161.3 0.0 copy-done
  161.3 0.0 copy-start.3
  161.3 0.9 convolution_convert_fusion.2
  162.2 0.0 reduce-scatter.5.cloned.1.call-update
  162.2 27.9 %reduce-scatter.5.cloned.1.call-done = bf16[16,768]{1,0:T(8,128)(2,1)} async-done(((bf16[128,768]{1,0:T(8,128)(2,1)}), bf16[16,768]{1,0:T(8,128)(2,1)}) %reduce-scatter.5.cloned.1.call-update) | async-done | bytes 24592 | tf_op jit(solution)/shard_map/reduce_scatter | solution.py:56
  190.2 0.0 copy-done.4
  190.2 0.7 add_maximum_fusion
  190.9 0.0 copy-done.5
  191.0 0.1 multiply_reduce_fusion
  191.1 0.0 copy-done.7
  191.1 0.7 copy.37
  191.7 0.0 copy-done.3
  (11 shorter events, 0.1 us)
Async XLA Ops:
  7.2 154.1 %copy-start = (bf16[192,768]{1,0:T(8,128)(2,1)S(1)}, bf16[192,768]{1,0:T(8,128)(2,1)}, u32[]{:S(2)}) copy-start(bf16[192,768]{1,0:T(8,128)(2,1)} %param.14) | copy-start | bytes 884740
  7.2 142.8 %reduce-scatter.7.cloned.1.call-start = ((), (), s32[]{:S(2)}) async-start(), calls=%async_computation.7 | async-start | bytes 1327104
  27.8 19.8 %copy-start.1 = (bf16[4,384,768]{2,1,0:T(8,128)(2,1)S(1)}, bf16[4,384,768]{2,1,0:T(8,128)(2,1)}, u32[]{:S(2)}) copy-start(bf16[4,384,768]{2,1,0:T(8,128)(2,1)} %param.12) | copy-start | bytes 7077892
  47.6 30.1 %copy-start.2 = (bf16[4,384,768]{2,1,0:T(8,128)(2,1)S(1)}, bf16[4,384,768]{2,1,0:T(8,128)(2,1)}, u32[]{:S(2)}) copy-start(bf16[4,384,768]{2,1,0:T(8,128)(2,1)} %param.13) | copy-start | bytes 7077892
  117.3 38.2 %copy-start.6 = (f32[128,2]{0,1:T(2,128)S(1)}, f32[128,2]{0,1:T(2,128)}, u32[]{:S(2)}) copy-start(f32[128,2]{0,1:T(2,128)} %param.11) | copy-start | bytes 3076
  117.3 72.9 %copy-start.4 = (f32[768]{0:T(1024)S(1)}, f32[768]{0:T(1024)}, u32[]{:S(2)}) copy-start(f32[768]{0:T(1024)} %param.15) | copy-start | bytes 9220
  117.3 73.7 %copy-start.5 = (f32[3,256]{1,0:T(4,128)S(1)}, f32[3,256]{1,0:T(4,128)}, u32[]{:S(2)}) copy-start(f32[3,256]{1,0:T(4,128)} %param.16) | copy-start | bytes 9220
  117.3 73.7 %copy-start.7 = (f32[3]{0:T(128)S(1)}, f32[3]{0:T(128)}, u32[]{:S(2)}) copy-start(f32[3]{0:T(128)} %param.17) | copy-start | bytes 40
  151.9 8.8 %all-to-all-start.3 = ((bf16[4,96,192]{2,1,0:T(8,128)(2,1)}), bf16[4,96,192]{2,1,0:T(8,128)(2,1)S(1)}, u32[]{:S(2)}, u32[]{:S(2)}) async-start(bf16[4,96,192]{2,1,0:T(8,128)(2,1)} %bitcast.13), calls=%async_computation.3 | async-start | bytes 393216 | tf_op jit(solution)/shard_map/all_to_all | solution.py:50
  155.5 34.7 %reduce-scatter.5.cloned.1.call-start = ((), (), s32[]{:S(2)}) async-start(), calls=%async_computation.6 | async-start | bytes 221184 | tf_op jit(solution)/shard_map/reduce_scatter | solution.py:56
  161.3 30.5 %copy-start.3 = (bf16[128,192]{0,1:T(8,128)(2,1)}, bf16[128,192]{0,1:T(8,128)(2,1)S(1)}, u32[]{:S(2)}) copy-start(bf16[128,192]{0,1:T(8,128)(2,1)S(1)} %fusion.3) | copy-start | bytes 147460
Sparse Core Ops, SparseCore 0:
  117.4 32.5 reduce-scatter.6
  162.4 27.7 reduce-scatter.4
where the time goes:
time: 199 us
  blocking collectives  95.8 us (48%)
  waiting for transfers between devices  65.8 us (33%)
  between operations  14.2 us (7%)
  local copies, waits for them, and re-layouts  8.73 us (4%)
  matrix products  7.42 us (4%)
  starting transfers between devices  3.68 us (2%)
  other arithmetic  2.92 us (1%)
    unnamed x3, waiting for transfers between devices  32.7 us
    all_to_all x1, blocking collectives, per_device(): lax.all_to_all(w_up, 'expert', split_axis=0, concat_axis=1, tiled=True)  30.1 us
    all_to_all x1, blocking collectives, per_device(): lax.all_to_all(w_down, 'expert', split_axis=0, concat_axis=1, tiled=True)  29.5 us
    reduce_scatter x1, waiting for transfers between devices, per_device(): lax.psum_scatter(jnp.dot(mixed, tower_in, preferred_element_type=jnp.floa...  27.9 us
    all_to_all x1, blocking collectives, per_device(): lax.all_to_all(outgoing, 'expert', split_axis=0, concat_axis=0, tiled=True)  19.8 us
    all_gather x1, blocking collectives, per_device(): full_rows = lax.all_gather(requests, ('tensor', 'rep'), axis=1, tiled=True)  16.4 us
    unnamed x22, local copies, waits for them, and re-layouts  7.94 us
    dot_general x1, matrix products, per_device(): jnp.einsum('sech,edh->secd', hidden, serve_down, preferred_element_type=j...  5.47 us
  transfers between devices with their start and end apart: 3, of which 3 were waited for; matrix products, arithmetic and copies ran while one was open for 0% of the time, Pallas kernels for 0%

commit v1 on v0

--- a/solution.py
+++ b/solution.py
@@ -2,6 +2,7 @@
 import jax.numpy as jnp
 from jax import lax
 from jax.sharding import PartitionSpec as P
+from jax.lax import axis_index, axis_size, ppermute
 
 
 def tower_head(pre, tower_bias, tower_out, out_bias):
@@ -34,7 +35,23 @@
     ).astype(jnp.bfloat16)
     full_rows = lax.all_gather(requests, ("tensor", "rep"), axis=1, tiled=True)
     outgoing = jnp.dot(spread, full_rows, preferred_element_type=jnp.float32).astype(jnp.bfloat16)
-    incoming = lax.all_to_all(outgoing, "expert", split_axis=0, concat_axis=0, tiled=True)
+    moved = axis_size("expert")
+    all_values = axis_index("expert")
+    front, heard = (moved, all_values)
+    b_now = outgoing.shape[0] // front
+    state_now = jnp.roll(outgoing, -heard * b_now, 0)
+    x_next = lax.slice_in_dim(state_now, 0, b_now, axis=0)
+    seen = [x_next]
+    for i0 in [*range(1, front)]:
+        state_next = lax.slice_in_dim(state_now, i0 * b_now, (i0 + 1) * b_now, axis=0)
+        tmp = ppermute(
+            state_next,
+            axis_name="expert",
+            perm=[(tick, (tick + i0) % front) for tick in range(front)],
+        )
+        seen.append(tmp)
+    val = jnp.concatenate(seen[::-1], 0)
+    incoming = jnp.roll(val, (heard + 1) * seen[0].shape[0], 0)
     shaped = incoming.reshape(groups, local_experts, capacity, incoming.shape[1])
     hidden_pre = jnp.einsum("secd,edh->sech", shaped, serve_up, preferred_element_type=jnp.float32)
     hidden = jax.nn.relu(hidden_pre).astype(jnp.bfloat16)

time: 199 us -> 184 us (0.925)
  blocking collectives: 95.8 us -> 15 us
  waiting for transfers between devices: 65.8 us -> 110 us
  starting transfers between devices: 3.68 us -> 17.5 us
  other arithmetic: 2.92 us -> 9.93 us
    all_to_all x3 -> x0, blocking collectives: 79.4 us -> none  [the longest x1 30.1 us: per_device(): lax.all_to_all(w_up, 'expert', split_axis=0, concat_axis=1, tiled=True)]
    all_to_all x0 -> x2, waiting for transfers between devices: none -> 25.4 us  [the longest x1 25.4 us: per_device(): lax.all_to_all(w_up, 'expert', split_axis=0, concat_axis=1, tiled=True)]
    ppermute x0 -> x3, waiting for transfers between devices: none -> 19 us  [per_device(): ppermute(state_next, axis_name='expert', perm=[(tick, (tick + i0) % front...]
    all_to_all x0 -> x2, starting transfers between devices: none -> 9.84 us  [the longest x1 5.34 us: per_device(): lax.all_to_all(w_up, 'expert', split_axis=0, concat_axis=1, tiled=True)]
    concatenate x0 -> x2, other arithmetic: none -> 7.7 us  [the longest x1 6.23 us: per_device(): incoming = jnp.roll(val, (heard + 1) * seen[0].shape[0], 0)]
    ppermute x0 -> x3, starting transfers between devices: none -> 3.91 us  [per_device(): ppermute(state_next, axis_name='expert', perm=[(tick, (tick + i0) % front...]
  transfers between devices with their start and end apart: 3 -> 8, of which waited for: 3 -> 6; matrix products, arithmetic and copies ran while one was open for 0% -> 6% of each run, Pallas kernels for 0% -> 0%
where the time goes in v1:
time: 184 us; the launch traced here: 183 us
  waiting for transfers between devices  110 us (60%)
  starting transfers between devices  17.5 us (10%)
  blocking collectives  15 us (8%)
  between operations  14.2 us (8%)
  other arithmetic  9.93 us (5%)
  local copies, waits for them, and re-layouts  8.92 us (5%)
  matrix products  7.45 us (4%)
    unnamed x3, waiting for transfers between devices  32.7 us
    reduce_scatter x1, waiting for transfers between devices, per_device(): lax.psum_scatter(jnp.dot(mixed, tower_in, preferred_element_type=jnp.floa...  27.8 us
    all_to_all x1, waiting for transfers between devices, per_device(): lax.all_to_all(w_up, 'expert', split_axis=0, concat_axis=1, tiled=True)  25.4 us
    ppermute x3, waiting for transfers between devices, per_device(): ppermute(state_next, axis_name='expert', perm=[(tick, (tick + i0) % front...  19 us
    all_gather x1, blocking collectives, per_device(): full_rows = lax.all_gather(requests, ('tensor', 'rep'), axis=1, tiled=True)  15 us
    unnamed x22, local copies, waits for them, and re-layouts  7.22 us
    concatenate x1, other arithmetic, per_device(): incoming = jnp.roll(val, (heard + 1) * seen[0].shape[0], 0)  6.23 us
    dot_general x1, matrix products, per_device(): jnp.einsum('sech,edh->secd', hidden, serve_down, preferred_element_type=j...  5.5 us
  transfers between devices with their start and end apart: 8, of which 6 were waited for; matrix products, arithmetic and copies ran while one was open for 6% of the time, Pallas kernels for 0%

profile of v1, /device:TPU:0, one launch (start us, length us, event | category | flops | bytes accessed | tf_op | source)
XLA Modules:
  0.0 183.1 jit_solution(1103523423884069744)
XLA Ops:
  7.2 0.0 copy-start
  7.2 5.3 %all-to-all-start = ((bf16[4,384,768]{2,1,0:T(8,128)(2,1)}), bf16[4,384,768]{2,1,0:T(8,128)(2,1)S(1)}, u32[]{:S(2)}, u32[]{:S(2)}) async-start(bf16[4,384,768]{2,1,0:T(8,128)(2,1)} %param.14), calls=%async_computation | async-start | bytes 4718592 | tf_op jit(solution)/shard_map/all_to_all | solution.py:24
  12.5 0.0 copy-done.3
  12.5 0.1 copy.32
  12.6 0.1 eq.87
  12.8 0.1 eq.83
  12.9 1.2 reduce-window.6
  14.2 0.1 slice.42
  14.2 0.1 copy.34
  14.4 0.1 copy.35
  14.5 0.1 add_bitcast_fusion
  14.6 0.1 reduce_sum.21
  14.7 0.1 copy.36
  14.8 0.0 copy-start.2
  14.8 25.4 %all-to-all-done = bf16[4,384,768]{2,1,0:T(8,128)(2,1)S(1)} async-done(((bf16[4,384,768]{2,1,0:T(8,128)(2,1)}), bf16[4,384,768]{2,1,0:T(8,128)(2,1)S(1)}, u32[]{:S(2)}, u32[]{:S(2)}) %all-to-all-start) | async-done | bytes 2359328 | tf_op jit(solution)/shard_map/all_to_all | solution.py:24
  40.2 4.5 %all-to-all-start.1 = ((bf16[4,384,768]{2,1,0:T(8,128)(2,1)}), bf16[4,384,768]{2,1,0:T(8,128)(2,1)}, u32[]{:S(2)}, u32[]{:S(2)}) async-start(bf16[4,384,768]{2,1,0:T(8,128)(2,1)} %param.15), calls=%async_computation.1 | async-start | bytes 4718592 | tf_op jit(solution)/shard_map/all_to_all | solution.py:25
  44.7 0.0 reduce-scatter.7.cloned.1.call-start
  44.8 15.0 %all_gather.3 = bf16[128,1536]{0,1:T(8,128)(2,1)S(1)} all-gather(bf16[128,192]{0,1:T(8,128)(2,1)S(1)} %copy-done.2), channel_id=1, replica_groups=mesh['expert'=4,'tensor'=4,'rep'=2] {'tensor','rep'}, dimensions={1}, use_global_device_ids=true | all-gather | bytes 442368 | tf_op jit(solution)/shard_map/all_gather | solution.py:36
  59.7 0.5 convolution_convert_fusion
  60.2 1.5 fusion.9
  61.7 0.9 fusion.23
  62.6 2.8 %collective-permute-start = (bf16[96,1536]{1,0:T(8,128)(2,1)}, bf16[96,1536]{1,0:T(8,128)(2,1)S(1)}, u32[]{:S(2)}, u32[]{:S(2)}) collective-permute-start(bf16[96,1536]{1,0:T(8,128)(2,1)} %get-tuple-element.10), channel_id=1, source_target_pairs={{0,24},{8,0},{16,8},{24,16},{1,25},{9,1},{17,9},{25,17},{2,26},{10... | collective-permute-start | bytes 884744 | tf_op jit(solution)/shard_map/ppermute | solution.py:47
  65.4 0.6 collective-permute-start.1
  65.9 0.6 collective-permute-start.2
  66.5 13.5 %collective-permute-done = bf16[96,1536]{1,0:T(8,128)(2,1)S(1)} collective-permute-done((bf16[96,1536]{1,0:T(8,128)(2,1)}, bf16[96,1536]{1,0:T(8,128)(2,1)S(1)}, u32[]{:S(2)}, u32[]{:S(2)}) %collective-permute-start) | collective-permute-done | bytes 294944 | tf_op jit(solution)/shard_map/ppermute | solution.py:47
  80.0 0.0 collective-permute-done.1
  80.0 5.5 %collective-permute-done.2 = bf16[96,1536]{1,0:T(8,128)(2,1)} collective-permute-done((bf16[96,1536]{1,0:T(8,128)(2,1)S(1)}, bf16[96,1536]{1,0:T(8,128)(2,1)}, u32[]{:S(2)}, u32[]{:S(2)}) %collective-permute-start.2) | collective-permute-done | bytes 294944 | tf_op jit(solution)/shard_map/ppermute | solution.py:47
  85.5 6.2 %fusion.5 = bf16[384,1536]{1,0:T(8,128)(2,1)} fusion(s32[]{:T(128)S(6)} %select_n.15, bf16[96,1536]{1,0:T(8,128)(2,1)S(1)} %collective-permute-done, bf16[96,1536]{1,0:T(8,128)(2,1)} %collective-permute-done.1, bf16[96,1536]{1,0:T(8,128)(2,1)} %collective-permute-done.2, bf16[96,1536]{1,0:T(8,128)(2,1)S(1)} %get-tuple-element.7), kind=kLoop, calls=%fused_computation.18 | loop fusion | flops 9437184 | bytes 2359300 | tf_op jit(solution)/shard_map/jit(_roll_dynamic)/concatenate | solution.py:54
  91.7 0.0 all-to-all-done.1
  91.7 5.5 %fusion = bf16[4,1,96,1536]{3,2,0,1:T(8,128)(2,1)} fusion(bf16[1536,768,1]{1,0,2:T(8,128)(2,1)} %bitcast.9, bf16[4,96,1536]{2,1,0:T(8,128)(2,1)} %bitcast.59, bf16[1536,768,1]{1,0,2:T(8,128)(2,1)S(1)} %bitcast.56), kind=kOutput, calls=%fused_computation.2 | convolution fusion | flops 1813118976 | bytes 7077888 | tf_op jit(solution)/shard_map/sech,edh->secd/dot_general | solution.py:58
  97.3 2.6 %copy.38 = bf16[4,1,96,1536]{2,0,1,3:T(4,128)(2,1)S(1)} copy(bf16[4,1,96,1536]{3,2,0,1:T(8,128)(2,1)} %fusion) | data formatting | bytes 2359296
  99.9 0.0 copy-start.6
  99.9 1.9 %reshape.69 = bf16[1536,384]{1,0:T(8,128)(2,1)} reshape(bf16[1536,1,4,96]{3,2,1,0:T(4,128)(2,1)S(1)} %bitcast.55) | data formatting | bytes 2359296
  101.8 0.0 reduce-scatter.7.cloned.1.call-update
  101.8 32.7 %reduce-scatter.7.cloned.1.call-done = bf16[192,384]{1,0:T(8,128)(2,1)} async-done(((bf16[1536,384]{1,0:T(8,128)(2,1)}), bf16[192,384]{1,0:T(8,128)(2,1)}) %reduce-scatter.7.cloned.1.call-update) | async-done | bytes 147472
  134.5 1.1 reshape.70
  135.5 0.8 copy.39
  136.4 3.7 %all-to-all-start.2 = ((bf16[4,96,192]{2,1,0:T(8,128)(2,1)}), bf16[4,96,192]{2,1,0:T(8,128)(2,1)S(1)}, u32[]{:S(2)}, u32[]{:S(2)}) async-start(bf16[4,96,192]{2,1,0:T(8,128)(2,1)} %bitcast.13), calls=%async_computation.2 | async-start | bytes 393216 | tf_op jit(solution)/shard_map/all_to_all | solution.py:67
  140.1 5.2 %all-to-all-done.2 = bf16[4,96,192]{2,1,0:T(8,128)(2,1)S(1)} async-done(((bf16[4,96,192]{2,1,0:T(8,128)(2,1)}), bf16[4,96,192]{2,1,0:T(8,128)(2,1)S(1)}, u32[]{:S(2)}, u32[]{:S(2)}) %all-to-all-start.2) | async-done | bytes 147488 | tf_op jit(solution)/shard_map/all_to_all | solution.py:67
  145.3 0.3 convolution_multiply_fusion
  145.6 0.3 fusion.11
  145.9 0.0 copy-start.1
  145.9 0.9 convolution_convert_fusion.2
  146.8 0.0 reduce-scatter.5.cloned.1.call-update
  146.8 27.8 %reduce-scatter.5.cloned.1.call-done = bf16[16,768]{1,0:T(8,128)(2,1)} async-done(((bf16[128,768]{1,0:T(8,128)(2,1)}), bf16[16,768]{1,0:T(8,128)(2,1)}) %reduce-scatter.5.cloned.1.call-update) | async-done | bytes 24592 | tf_op jit(solution)/shard_map/reduce_scatter | solution.py:73
  174.7 0.7 add_maximum_fusion
  175.5 0.1 multiply_reduce_fusion
  175.6 0.7 copy.37
  (21 shorter events, 0.2 us)
Async XLA Ops:
  7.2 138.7 %copy-start = (bf16[192,768]{1,0:T(8,128)(2,1)S(1)}, bf16[192,768]{1,0:T(8,128)(2,1)}, u32[]{:S(2)}) copy-start(bf16[192,768]{1,0:T(8,128)(2,1)} %param.16) | copy-start | bytes 884740
  7.2 5.3 %copy-start.3 = (s32[128,2]{0,1:T(2,128)S(1)}, s32[128,2]{0,1:T(2,128)}, u32[]{:S(2)}) copy-start(s32[128,2]{0,1:T(2,128)} %param.12) | copy-start | bytes 3076
  7.2 33.0 %all-to-all-start = ((bf16[4,384,768]{2,1,0:T(8,128)(2,1)}), bf16[4,384,768]{2,1,0:T(8,128)(2,1)S(1)}, u32[]{:S(2)}, u32[]{:S(2)}) async-start(bf16[4,384,768]{2,1,0:T(8,128)(2,1)} %param.14), calls=%async_computation | async-start | bytes 4718592 | tf_op jit(solution)/shard_map/all_to_all | solution.py:24
  14.8 30.0 %copy-start.2 = (bf16[128,192]{0,1:T(8,128)(2,1)S(1)}, bf16[128,192]{0,1:T(8,128)(2,1)}, u32[]{:S(2)}) copy-start(bf16[128,192]{0,1:T(8,128)(2,1)} %param.11) | copy-start | bytes 147460
  40.2 51.5 %all-to-all-start.1 = ((bf16[4,384,768]{2,1,0:T(8,128)(2,1)}), bf16[4,384,768]{2,1,0:T(8,128)(2,1)}, u32[]{:S(2)}, u32[]{:S(2)}) async-start(bf16[4,384,768]{2,1,0:T(8,128)(2,1)} %param.15), calls=%async_computation.1 | async-start | bytes 4718592 | tf_op jit(solution)/shard_map/all_to_all | solution.py:25
  44.7 89.8 %reduce-scatter.7.cloned.1.call-start = ((), (), s32[]{:S(2)}) async-start(), calls=%async_computation.6 | async-start | bytes 1327104
  62.6 17.4 %collective-permute-start = (bf16[96,1536]{1,0:T(8,128)(2,1)}, bf16[96,1536]{1,0:T(8,128)(2,1)S(1)}, u32[]{:S(2)}, u32[]{:S(2)}) collective-permute-start(bf16[96,1536]{1,0:T(8,128)(2,1)} %get-tuple-element.10), channel_id=1, source_target_pairs={{0,24},{8,0},{16,8},{24,16},{1,25},{9,1},{17,9},{25,17},{2,26},{10... | collective-permute-start | bytes 884744 | tf_op jit(solution)/shard_map/ppermute | solution.py:47
  65.4 14.6 %collective-permute-start.1 = (bf16[96,1536]{1,0:T(8,128)(2,1)}, bf16[96,1536]{1,0:T(8,128)(2,1)}, u32[]{:S(2)}, u32[]{:S(2)}) collective-permute-start(bf16[96,1536]{1,0:T(8,128)(2,1)} %get-tuple-element.9), channel_id=1, source_target_pairs={{0,16},{8,24},{16,0},{24,8},{1,17},{9,25},{17,1},{25,9},{2,18},{10... | collective-permute-start | bytes 884744 | tf_op jit(solution)/shard_map/ppermute | solution.py:47
  65.9 19.6 %collective-permute-start.2 = (bf16[96,1536]{1,0:T(8,128)(2,1)S(1)}, bf16[96,1536]{1,0:T(8,128)(2,1)}, u32[]{:S(2)}, u32[]{:S(2)}) collective-permute-start(bf16[96,1536]{1,0:T(8,128)(2,1)S(1)} %get-tuple-element.8), channel_id=1, source_target_pairs={{0,8},{8,16},{16,24},{24,0},{1,9},{9,17},{17,25},{25,1},{2,10},{10... | collective-permute-start | bytes 884744 | tf_op jit(solution)/shard_map/ppermute | solution.py:47
  99.9 40.2 %copy-start.6 = (f32[128,2]{0,1:T(2,128)S(1)}, f32[128,2]{0,1:T(2,128)}, u32[]{:S(2)}) copy-start(f32[128,2]{0,1:T(2,128)} %param.13) | copy-start | bytes 3076
  101.8 72.9 %copy-start.4 = (f32[768]{0:T(1024)S(1)}, f32[768]{0:T(1024)}, u32[]{:S(2)}) copy-start(f32[768]{0:T(1024)} %param.17) | copy-start | bytes 9220
  101.8 73.7 %copy-start.5 = (f32[3,256]{1,0:T(4,128)S(1)}, f32[3,256]{1,0:T(4,128)}, u32[]{:S(2)}) copy-start(f32[3,256]{1,0:T(4,128)} %param.18) | copy-start | bytes 9220
  101.8 73.8 %copy-start.7 = (f32[3]{0:T(128)S(1)}, f32[3]{0:T(128)}, u32[]{:S(2)}) copy-start(f32[3]{0:T(128)} %param.19) | copy-start | bytes 40
  136.4 8.9 %all-to-all-start.2 = ((bf16[4,96,192]{2,1,0:T(8,128)(2,1)}), bf16[4,96,192]{2,1,0:T(8,128)(2,1)S(1)}, u32[]{:S(2)}, u32[]{:S(2)}) async-start(bf16[4,96,192]{2,1,0:T(8,128)(2,1)} %bitcast.13), calls=%async_computation.2 | async-start | bytes 393216 | tf_op jit(solution)/shard_map/all_to_all | solution.py:67
  140.1 34.6 %reduce-scatter.5.cloned.1.call-start = ((), (), s32[]{:S(2)}) async-start(), calls=%async_computation.5 | async-start | bytes 221184 | tf_op jit(solution)/shard_map/reduce_scatter | solution.py:73
  145.9 30.4 %copy-start.1 = (bf16[128,192]{0,1:T(8,128)(2,1)}, bf16[128,192]{0,1:T(8,128)(2,1)S(1)}, u32[]{:S(2)}) copy-start(bf16[128,192]{0,1:T(8,128)(2,1)S(1)} %fusion.11) | copy-start | bytes 147460
Sparse Core Ops, SparseCore 0:
  101.9 32.4 reduce-scatter.6
  146.9 27.6 reduce-scatter.4
